TPU v7x, 256 devices: a whole 4x4x8 slice. The times are simulated.
256 devices in a mesh: expert: 16 (over x, y), dp: 16 (over z, core).
Axes of the slice: x: 4, y: 4, z: 8, core: 2. Of those that a mesh axis runs over, the one named last changes fastest.
Arguments:
- tokens: bfloat16 [2, 32768, 1280], P(None, ('expert', 'dp')), may hold values from -6 to 6
- modality: int32 [2, 32768], P(None, ('expert', 'dp')), may hold values from 0 to 1, as said below
- routes: int32 [2, 32768, 1], P(None, ('expert', 'dp')), may hold values from 0 to 15; in each aligned block of 128 rows (0 to 127, 128 to 255, ..., all dimensions but the last counted through in order) at most 16 rows name the same one
- router: bfloat16 [1280, 16], replicated, may hold values from -0.15625 to 0.15625
- w_in: bfloat16 [16, 1280, 5120], P('expert', 'dp'), may hold values from -0.15625 to 0.15625
- w_out: bfloat16 [16, 5120, 1280], P('expert', 'dp'), may hold values from -0.078125 to 0.078125
Outputs:
- mixed: bfloat16 [2, 32768, 1280], P(None, ('expert', 'dp'))
- load: float32 [2, 2, 16], replicated
Inputs may be any that keep to these rules, and one draw needn't show every extreme that they name: `routes`: among the 128 tokens of one micro-batch on one device (aligned blocks of 128 rows), at most 16 are routed to any one expert. `modality`: in every aligned block of 128 tokens of a micro-batch, the number of text tokens lies between 32 and 96.
All inputs are finite; a program needn't handle non-finite values.
Results may differ from a plain program's by a relative error of at most 0.0057.
Values may be sent and summed in bfloat16 or wider, within the bound.
No kernel may reach another device: no remote copies, remote signals or barrier semaphores. Data moves between devices by JAX's collectives and lax.ppermute only.
A program may use at most 192 MiB of HBM per device.

v0:
```python
import jax
import jax.numpy as jnp
from jax import lax
from jax.sharding import Mesh
from jax.sharding import PartitionSpec as P

EXPERT = ("expert_0", "expert_1")
DP = ("dp_0", "dp_1")
EXPERT_DP = ("expert_0", "expert_1", "dp_0", "dp_1")


def over_axes(shard, axes):
    for axis in axes:
        shard = lax.psum(shard, axis)
    return shard


def on_device(tokens, modality, routes, router, w_in, w_out):
    micro_count, tok_count, model_width = tokens.shape
    experts = router.shape[1]
    capacity = 2 * tok_count // experts
    logits = jnp.einsum("mtd,de->mte", tokens, router, preferred_element_type=jnp.float32)
    onehot = (routes == jnp.arange(experts, dtype=jnp.int32)[None, None, :]).astype(jnp.float32)
    gating = jax.nn.sigmoid(jnp.sum(logits * onehot, axis=-1))
    running = jnp.cumsum(onehot, axis=1)
    slot_pos = jnp.sum((running - 1.0) * onehot, axis=-1)
    slot_hot = (
        slot_pos[:, :, None] == jnp.arange(capacity, dtype=jnp.float32)[None, None, :]
    ).astype(jnp.float32)
    placer = (onehot[:, :, :, None] * slot_hot[:, :, None, :]).reshape(
        micro_count, tok_count, experts * capacity
    )
    placer = placer.astype(jnp.bfloat16)
    buffer = jnp.einsum("mtk,mtd->mkd", placer, tokens, preferred_element_type=jnp.float32)
    buffer = buffer.astype(jnp.bfloat16).reshape(micro_count, experts, capacity, model_width)
    arrived = lax.all_to_all(buffer, EXPERT, split_axis=1, concat_axis=1, tiled=True)
    token_rows = arrived.reshape(-1, model_width)
    columns = token_rows
    pre_act = jnp.dot(
        columns, lax.all_gather(w_in, DP, axis=1, tiled=True)[0], preferred_element_type=jnp.float32
    )
    hidden = jax.nn.gelu(pre_act, approximate=True).astype(jnp.bfloat16)
    columns = hidden
    served = jnp.dot(
        columns,
        lax.all_gather(w_out, DP, axis=1, tiled=True)[0],
        preferred_element_type=jnp.float32,
    )
    served = served.astype(jnp.bfloat16).reshape(arrived.shape)
    returned = lax.all_to_all(served, EXPERT, split_axis=1, concat_axis=1, tiled=True)
    returned = returned.reshape(micro_count, experts * capacity, model_width)
    combined = jnp.einsum("mtk,mkd->mtd", placer, returned, preferred_element_type=jnp.float32)
    mixed = (combined * gating[:, :, None]).astype(jnp.bfloat16)
    exps = jnp.exp(logits)
    router_probs = exps / jnp.sum(exps, axis=-1, keepdims=True)
    modal_hot = (modality[:, :, None] == jnp.arange(2, dtype=jnp.int32)[None, None, :]).astype(
        jnp.float32
    )
    counts = jnp.einsum("mtk,mte->ke", modal_hot, onehot, precision=lax.Precision.HIGHEST)
    prob_sums = jnp.einsum("mtk,mte->ke", modal_hot, router_probs, precision=lax.Precision.HIGHEST)
    modal_counts = jnp.sum(modal_hot, axis=(0, 1))
    counts, prob_sums, modal_counts = (
        over_axes(counts, EXPERT_DP),
        over_axes(prob_sums, EXPERT_DP),
        over_axes(modal_counts, EXPERT_DP),
    )
    load = jnp.stack(
        [experts * counts / modal_counts[:, None], experts * prob_sums / modal_counts[:, None]]
    )
    return (mixed, load)


def solution(mesh):
    torus = Mesh(mesh.devices.reshape(4, 4, 8, 2), ("expert_0", "expert_1", "dp_0", "dp_1"))
    in_specs = (
        P(None, EXPERT_DP, None),
        P(None, EXPERT_DP),
        P(None, EXPERT_DP, None),
        P(),
        P(EXPERT, DP, None),
        P(EXPERT, DP, None),
    )
    out_specs = (P(None, EXPERT_DP, None), P())
    return jax.shard_map(
        on_device, mesh=torus, in_specs=in_specs, out_specs=out_specs, check_vma=False
    )
```

profile of v0, /device:TPU:1, one launch (start us, length us, event | category | flops | bytes accessed | tf_op | source)
XLA Modules:
  0.0 258.7 jit_solution(4837752513307506845)
XLA Ops:
  7.2 0.0 copy-start
  7.2 0.0 all-gather.5.cloned.1.call-start
  7.2 0.7 all-gather.5.cloned.1.call-update
  7.9 0.0 all-gather.3.cloned.1.call-start
  8.0 0.7 all-gather.3.cloned.1.call-update
  8.7 0.7 fusion.30
  9.3 0.1 copy.21
  9.5 0.2 reduce_window_sum.11
  9.6 0.1 copy.22
  9.7 0.8 fusion.29
  10.5 0.5 convolution_convert_fusion
  11.0 0.1 copy.23
  11.1 26.3 %all_to_all.10 = bf16[2,16,16,1280]{3,2,0,1:T(8,128)(2,1)S(1)} all-to-all(bf16[2,16,16,1280]{3,2,0,1:T(8,128)(2,1)S(1)} %copy.23), channel_id=1, replica_groups=mesh['expert_0'=4,'expert_1'=4,'dp_0'=8,'dp_1'=2] {'expert_0','expert_1'}, dimensions={1} | all-to-all | bytes 2621440 | tf_op jit(solution)/shard_map/all_to_all | solution.py:36
  37.5 0.1 copy.24
  37.6 54.6 %all-gather.5.cloned.1.call-done = bf16[1,5120,1280]{2,1,0:T(8,128)(2,1)} async-done(((bf16[1,320,1280]{2,1,0:T(8,128)(2,1)}), bf16[1,5120,1280]{2,1,0:T(8,128)(2,1)}) %all-gather.5.cloned.1.call-update) | async-done | bytes 13107216 | tf_op jit(solution)/shard_map/all_gather | solution.py:46
  92.1 78.5 %all-gather.3.cloned.1.call-done = bf16[1,1280,5120]{2,1,0:T(8,128)(2,1)} async-done(((bf16[1,80,5120]{2,1,0:T(8,128)(2,1)}), bf16[1,1280,5120]{2,1,0:T(8,128)(2,1)}) %all-gather.3.cloned.1.call-update) | async-done | bytes 13107216 | tf_op jit(solution)/shard_map/all_gather | solution.py:40
  170.6 22.4 %fusion.20 = bf16[512,1280]{1,0:T(8,128)(2,1)S(1)} fusion(bf16[1,5120,1280]{2,1,0:T(8,128)(2,1)} %all-gather.5.cloned.1.call-done, bf16[512,1280]{1,0:T(8,128)(2,1)S(1)} %bitcast.41, bf16[1,1280,5120]{2,1,0:T(8,128)(2,1)} %all-gather.3.cloned.1.call-done), kind=kOutput, calls=%fused_computation.17 | convolution fusion | flops 13446021120 | bytes 28835840 | tf_op jit(solution)/shard_map/dot_general | solution.py:44
  193.0 0.0 copy-start.3
  193.0 1.2 copy.25
  194.2 6.5 %all-to-all-start.1 = ((bf16[2,16,16,1280]{3,2,0,1:T(8,128)(2,1)}), bf16[2,16,16,1280]{3,2,0,1:T(8,128)(2,1)S(1)}, u32[]{:S(2)}, u32[]{:S(2)}) async-start(bf16[2,16,16,1280]{3,2,0,1:T(8,128)(2,1)} %copy.25), calls=%async_computation.1 | async-start | bytes 2621440 | tf_op jit(solution)/shard_map/all_to_all | solution.py:50
  200.8 0.1 convert_reduce_fusion
  200.9 0.1 convolution_bitcast_fusion.1
  201.0 0.3 exponential_reduce_fusion
  201.4 0.1 convolution_bitcast_fusion
  201.5 18.4 %all-reduce.2 = (f32[2,16]{1,0:T(2,128)S(1)}, f32[2]{0:T(128)S(1)}, f32[2,16]{1,0:T(2,128)S(1)}) all-reduce(f32[2,16]{1,0:T(2,128)S(1)} %convolution_bitcast_fusion, f32[2]{0:T(128)S(1)} %convert_reduce_fusion, f32[2,16]{1,0:T(2,128)S(1)} %convolution_bitcast_fusion.1), channel_id=1, replica_groups=mesh['expert_0'=4,'expert_1'=4,'dp_0'=8,'dp_1'=2] {'expert_0'}, use_global_device_ids=true, to_apply=%region_13.14 | all-reduce | flops 66 | bytes 528 | tf_op jit(solution)/shard_map/psum | solution.py:14
  219.9 8.1 %all-reduce.1 = (f32[2,16]{1,0:T(2,128)S(1)}, f32[2]{0:T(128)S(1)}, f32[2,16]{1,0:T(2,128)S(1)}) all-reduce(f32[2,16]{1,0:T(2,128)S(1)} %get-tuple-element.10, f32[2]{0:T(128)S(1)} %get-tuple-element.11, f32[2,16]{1,0:T(2,128)S(1)} %get-tuple-element.12), channel_id=1, replica_groups=mesh['expert_0'=4,'expert_1'=4,'dp_0'=8,'dp_1'=2] {'expert_1'}, use_global_device_ids=true, to_apply=%region_14.15 | all-reduce | flops 66 | bytes 528 | tf_op jit(solution)/shard_map/psum | solution.py:14
  227.9 11.8 %all-reduce = (f32[2,16]{1,0:T(2,128)S(1)}, f32[2]{0:T(128)S(1)}, f32[2,16]{1,0:T(2,128)S(1)}) all-reduce(f32[2,16]{1,0:T(2,128)S(1)} %get-tuple-element.7, f32[2]{0:T(128)S(1)} %get-tuple-element.8, f32[2,16]{1,0:T(2,128)S(1)} %get-tuple-element.9), channel_id=1, replica_groups=mesh['expert_0'=4,'expert_1'=4,'dp_0'=8,'dp_1'=2] {'dp_0'}, use_global_device_ids=true, to_apply=%region_15.16 | all-reduce | flops 66 | bytes 528 | tf_op jit(solution)/shard_map/psum | solution.py:14
  239.7 10.2 %all-reduce.3 = (f32[2,16]{1,0:T(2,128)S(1)}, f32[2]{0:T(128)S(1)}, f32[2,16]{1,0:T(2,128)S(1)}) all-reduce(f32[2,16]{1,0:T(2,128)S(1)} %get-tuple-element.4, f32[2]{0:T(128)S(1)} %get-tuple-element.5, f32[2,16]{1,0:T(2,128)S(1)} %get-tuple-element.6), channel_id=1, replica_groups=mesh['expert_0'=4,'expert_1'=4,'dp_0'=8,'dp_1'=2] {'dp_1'}, use_global_device_ids=true, to_apply=%region_16.17 | all-reduce | flops 66 | bytes 528 | tf_op jit(solution)/shard_map/psum | solution.py:14
  249.9 0.1 divide_bitcast_fusion.1
  249.9 0.6 pad_maximum_fusion
  250.5 0.1 copy.26
  250.6 1.2 fusion.25
  (9 shorter events, 0.1 us)
Async XLA Ops:
  7.2 3.3 %copy-start = (bf16[2,128,1280]{2,1,0:T(8,128)(2,1)S(1)}, bf16[2,128,1280]{2,1,0:T(8,128)(2,1)}, u32[]{:S(2)}) copy-start(bf16[2,128,1280]{2,1,0:T(8,128)(2,1)} %param.6) | copy-start | bytes 1966084
  7.2 84.9 %all-gather.5.cloned.1.call-start = ((), (), s32[]{:S(2)}) async-start(), calls=%async_computation.3 | async-start | bytes 13926400 | tf_op jit(solution)/shard_map/all_gather | solution.py:46
  7.9 162.7 %all-gather.3.cloned.1.call-start = ((), (), s32[]{:S(2)}) async-start(), calls=%async_computation.2 | async-start | bytes 13926400 | tf_op jit(solution)/shard_map/all_gather | solution.py:40
  193.0 7.8 %copy-start.3 = (s32[2,128]{1,0:T(2,128)S(1)}, s32[2,128]{1,0:T(2,128)}, u32[]{:S(2)}) copy-start(s32[2,128]{1,0:T(2,128)} %param.7) | copy-start | bytes 3076
  193.0 7.9 %copy-start.2 = (s32[2,128,1]{1,2,0:T(1,128)S(1)}, s32[2,128,1]{1,2,0:T(1,128)}, u32[]{:S(2)}) copy-start(s32[2,128,1]{1,2,0:T(1,128)} %param.8) | copy-start | bytes 3076
  193.0 8.0 %copy-start.1 = (bf16[1280,16]{0,1:T(8,128)(2,1)S(1)}, bf16[1280,16]{0,1:T(8,128)(2,1)}, u32[]{:S(2)}) copy-start(bf16[1280,16]{0,1:T(8,128)(2,1)} %param.9) | copy-start | bytes 122884
  194.2 56.3 %all-to-all-start.1 = ((bf16[2,16,16,1280]{3,2,0,1:T(8,128)(2,1)}), bf16[2,16,16,1280]{3,2,0,1:T(8,128)(2,1)S(1)}, u32[]{:S(2)}, u32[]{:S(2)}) async-start(bf16[2,16,16,1280]{3,2,0,1:T(8,128)(2,1)} %copy.25), calls=%async_computation.1 | async-start | bytes 2621440 | tf_op jit(solution)/shard_map/all_to_all | solution.py:50
Sparse Core Ops, SparseCore 0:
  9.8 82.2 all-gather.4
  93.9 76.5 all-gather.2
where the time goes:
time: 259 us
  waiting for transfers between devices  134 us (52%)
  blocking collectives  74.7 us (29%)
  matrix products  24.7 us (10%)
  between operations  14.2 us (5%)
  starting transfers between devices  6.6 us (3%)
    all_gather x1, waiting for transfers between devices, on_device(): lax.all_gather(w_in, DP, axis=1, tiled=True)[0]  78.5 us
    all_gather x1, waiting for transfers between devices, on_device(): lax.all_gather(w_out, DP, axis=1, tiled=True)[0]  54.6 us
    psum x4, blocking collectives, over_axes(): shard = lax.psum(shard, axis)  48.4 us
    all_to_all x1, blocking collectives, on_device(): lax.all_to_all(buffer, EXPERT, split_axis=1, concat_axis=1, tiled=True)  26.3 us
    dot_general x1, matrix products, on_device(): jnp.dot(columns, lax.all_gather(w_out, DP, axis=1, tiled=True)[0], prefer...  22.4 us
    all_to_all x1, starting transfers between devices, on_device(): lax.all_to_all(served, EXPERT, split_axis=1, concat_axis=1, tiled=True)  6.52 us
  transfers between devices with their start and end apart: 3, of which 2 were waited for; matrix products, arithmetic and copies ran while one was open for 2% of the time, Pallas kernels for 0%

commit v1 on v0

--- a/solution.py
+++ b/solution.py
@@ -3,15 +3,21 @@
 from jax import lax
 from jax.sharding import Mesh
 from jax.sharding import PartitionSpec as P
+from jax.lax import all_gather
 
 EXPERT = ("expert_0", "expert_1")
 DP = ("dp_0", "dp_1")
 EXPERT_DP = ("expert_0", "expert_1", "dp_0", "dp_1")
 
 
+def fill_layers_all(sample, ax_name):
+    last = jnp.sum(all_gather(sample, ax_name), axis=0)
+    return last
+
+
 def over_axes(shard, axes):
     for axis in axes:
-        shard = lax.psum(shard, axis)
+        shard = fill_layers_all(shard, axis)
     return shard
 
 

time: 259 us -> 290 us (1.12)
  blocking collectives: 74.7 us -> 131 us
  waiting for transfers between devices: 134 us -> 93.1 us
  starting transfers between devices: 6.6 us -> 14.2 us
  local copies, waits for them, and re-layouts: 1.69 us -> 6.42 us
    all_gather x0 -> x8, blocking collectives: none -> 78.1 us  [fill_layers_all(): last = jnp.sum(all_gather(sample, ax_name), axis=0)]
    unnamed x0 -> x4, blocking collectives: none -> 52.9 us
    psum x4 -> x0, blocking collectives: 48.4 us -> none  [over_axes(): shard = lax.psum(shard, axis)]
    all_gather x1, waiting for transfers between devices: 54.6 us -> 13.3 us  [on_device(): lax.all_gather(w_out, DP, axis=1, tiled=True)[0]]
    all_to_all x1 -> x0, blocking collectives: 26.3 us -> none  [on_device(): lax.all_to_all(buffer, EXPERT, split_axis=1, concat_axis=1, tiled=True)]
    all_to_all x0 -> x1, starting transfers between devices: none -> 7.57 us  [on_device(): lax.all_to_all(buffer, EXPERT, split_axis=1, concat_axis=1, tiled=True)]
    unnamed x8 -> x28, local copies, waits for them, and re-layouts: 0.03 us -> 3.37 us
  transfers between devices with their start and end apart: 3 -> 4, of which waited for: 2 -> 2; matrix products, arithmetic and copies ran while one was open for 2% -> 3% of each run, Pallas kernels for 0% -> 0%
where the time goes in v1:
time: 290 us; the launch traced here: 289 us
  blocking collectives  131 us (45%)
  waiting for transfers between devices  93.1 us (32%)
  matrix products  24.9 us (9%)
  between operations  16.9 us (6%)
  starting transfers between devices  14.2 us (5%)
  local copies, waits for them, and re-layouts  6.42 us (2%)
    all_gather x1, waiting for transfers between devices, on_device(): lax.all_gather(w_in, DP, axis=1, tiled=True)[0]  78.5 us
    all_gather x8, blocking collectives, fill_layers_all(): last = jnp.sum(all_gather(sample, ax_name), axis=0)  78.1 us
    unnamed x4, blocking collectives  52.9 us
    dot_general x1, matrix products, on_device(): jnp.dot(columns, lax.all_gather(w_out, DP, axis=1, tiled=True)[0], prefer...  22.6 us
    all_gather x1, waiting for transfers between devices, on_device(): lax.all_gather(w_out, DP, axis=1, tiled=True)[0]  13.3 us
    all_to_all x1, starting transfers between devices, on_device(): lax.all_to_all(buffer, EXPERT, split_axis=1, concat_axis=1, tiled=True)  7.57 us
    all_to_all x1, starting transfers between devices, on_device(): lax.all_to_all(served, EXPERT, split_axis=1, concat_axis=1, tiled=True)  6.53 us
  transfers between devices with their start and end apart: 4, of which 2 were waited for; matrix products, arithmetic and copies ran while one was open for 3% of the time, Pallas kernels for 0%

profile of v1, /device:TPU:1, one launch (start us, length us, event | category | flops | bytes accessed | tf_op | source)
XLA Modules:
  0.0 289.1 jit_solution(3611102309069886487)
XLA Ops:
  7.3 0.7 all-gather.25.cloned.1.call-update
  8.0 0.7 all-gather.23.cloned.1.call-update
  8.7 0.7 fusion.30
  9.8 0.8 fusion.29
  10.6 0.5 convolution_convert_fusion
  11.1 1.2 copy.23
  12.2 7.6 %all-to-all-start = ((bf16[2,16,16,1280]{3,2,0,1:T(8,128)(2,1)}), bf16[2,16,16,1280]{3,2,0,1:T(8,128)(2,1)S(1)}, u32[]{:S(2)}, u32[]{:S(2)}) async-start(bf16[2,16,16,1280]{3,2,0,1:T(8,128)(2,1)} %copy.23), calls=%async_computation | async-start | bytes 2621440 | tf_op jit(solution)/shard_map/all_to_all | solution.py:42
  19.8 0.6 dynamic-slice
  21.4 17.2 %all-reduce = f32[8]{0:T(128)S(1)} all-reduce(f32[8]{0:T(128)S(1)} %dynamic-update-slice), channel_id=6, replica_groups=mesh['expert_0'=4,'expert_1'=4,'dp_0'=8,'dp_1'=2] {'expert_0'}, use_global_device_ids=true, to_apply=%add | all-reduce | flops 8 | bytes 64
  38.8 0.6 dynamic-slice.1
  40.3 9.3 %all-reduce.1 = f32[8]{0:T(128)S(1)} all-reduce(f32[8]{0:T(128)S(1)} %dynamic-update-slice.1), channel_id=7, replica_groups=mesh['expert_0'=4,'expert_1'=4,'dp_0'=8,'dp_1'=2] {'expert_1'}, use_global_device_ids=true, to_apply=%add.1 | all-reduce | flops 8 | bytes 64
  49.6 0.6 dynamic-slice.2
  50.9 0.2 dynamic-update-slice.2
  51.1 18.7 %all-reduce.2 = f32[16]{0:T(128)S(1)} all-reduce(f32[16]{0:T(128)S(1)} %dynamic-update-slice.2), channel_id=8, replica_groups=mesh['expert_0'=4,'expert_1'=4,'dp_0'=8,'dp_1'=2] {'dp_0'}, use_global_device_ids=true, to_apply=%add.2 | all-reduce | flops 16 | bytes 128
  69.9 0.6 dynamic-slice.3
  71.4 7.7 %all-reduce.3 = f32[4]{0:T(128)S(1)} all-reduce(f32[4]{0:T(128)S(1)} %dynamic-update-slice.3), channel_id=9, replica_groups=mesh['expert_0'=4,'expert_1'=4,'dp_0'=8,'dp_1'=2] {'dp_1'}, use_global_device_ids=true, to_apply=%add.3 | all-reduce | flops 4 | bytes 32
  79.3 13.3 %all-gather.25.cloned.1.call-done = bf16[1,5120,1280]{2,1,0:T(8,128)(2,1)} async-done(((bf16[1,320,1280]{2,1,0:T(8,128)(2,1)}), bf16[1,5120,1280]{2,1,0:T(8,128)(2,1)}) %all-gather.25.cloned.1.call-update) | async-done | bytes 13107216 | tf_op jit(solution)/shard_map/all_gather | solution.py:52
  92.5 78.5 %all-gather.23.cloned.1.call-done = bf16[1,1280,5120]{2,1,0:T(8,128)(2,1)} async-done(((bf16[1,80,5120]{2,1,0:T(8,128)(2,1)}), bf16[1,1280,5120]{2,1,0:T(8,128)(2,1)}) %all-gather.23.cloned.1.call-update) | async-done | bytes 13107216 | tf_op jit(solution)/shard_map/all_gather | solution.py:46
  171.0 22.6 %fusion.20 = bf16[512,1280]{1,0:T(8,128)(2,1)S(1)} fusion(bf16[1,5120,1280]{2,1,0:T(8,128)(2,1)} %all-gather.25.cloned.1.call-done, bf16[512,1280]{1,0:T(8,128)(2,1)S(1)} %bitcast.53, bf16[1,1280,5120]{2,1,0:T(8,128)(2,1)} %all-gather.23.cloned.1.call-done), kind=kOutput, calls=%fused_computation.17 | convolution fusion | flops 13446021120 | bytes 28835840 | tf_op jit(solution)/shard_map/dot_general | solution.py:50
  193.6 1.2 copy.25
  194.8 6.5 %all-to-all-start.1 = ((bf16[2,16,16,1280]{3,2,0,1:T(8,128)(2,1)}), bf16[2,16,16,1280]{3,2,0,1:T(8,128)(2,1)S(1)}, u32[]{:S(2)}, u32[]{:S(2)}) async-start(bf16[2,16,16,1280]{3,2,0,1:T(8,128)(2,1)} %copy.25), calls=%async_computation.1 | async-start | bytes 2621440 | tf_op jit(solution)/shard_map/all_to_all | solution.py:56
  201.5 18.5 %all-gather.12 = f32[4,2,16]{2,1,0:T(2,128)S(1)} all-gather(f32[1,2,16]{2,1,0:T(2,128)S(1)} %convolution_bitcast_fusion.1), channel_id=2, replica_groups=mesh['expert_0'=4,'expert_1'=4,'dp_0'=8,'dp_1'=2] {'expert_0'}, dimensions={0}, use_global_device_ids=true | all-gather | bytes 640 | tf_op jit(solution)/shard_map/all_gather | solution.py:14
  220.1 7.6 %all-gather.13 = f32[4,2,16]{2,1,0:T(2,128)S(1)} all-gather(f32[1,2,16]{2,1,0:T(2,128)S(1)} %bitcast.63), channel_id=3, replica_groups=mesh['expert_0'=4,'expert_1'=4,'dp_0'=8,'dp_1'=2] {'expert_1'}, dimensions={0}, use_global_device_ids=true | all-gather | bytes 640 | tf_op jit(solution)/shard_map/all_gather | solution.py:14
  227.7 10.9 %all-gather.14 = f32[8,2,16]{2,1,0:T(2,128)S(1)} all-gather(f32[1,2,16]{2,1,0:T(2,128)S(1)} %bitcast.64), channel_id=4, replica_groups=mesh['expert_0'=4,'expert_1'=4,'dp_0'=8,'dp_1'=2] {'dp_0'}, dimensions={0}, use_global_device_ids=true | all-gather | bytes 1152 | tf_op jit(solution)/shard_map/all_gather | solution.py:14
  238.6 9.5 %all-gather.15 = f32[2,2,16]{2,1,0:T(2,128)S(1)} all-gather(f32[1,2,16]{2,1,0:T(2,128)S(1)} %bitcast.61), channel_id=5, replica_groups=mesh['expert_0'=4,'expert_1'=4,'dp_0'=8,'dp_1'=2] {'dp_1'}, dimensions={0}, use_global_device_ids=true | all-gather | bytes 384 | tf_op jit(solution)/shard_map/all_gather | solution.py:14
  248.2 0.3 exponential_reduce_fusion
  248.7 6.7 %all-gather.16 = f32[4,2,16]{2,1,0:T(2,128)S(1)} all-gather(f32[1,2,16]{2,1,0:T(2,128)S(1)} %convolution_bitcast_fusion), channel_id=10, replica_groups=mesh['expert_0'=4,'expert_1'=4,'dp_0'=8,'dp_1'=2] {'expert_0'}, dimensions={0}, use_global_device_ids=true | all-gather | bytes 640 | tf_op jit(solution)/shard_map/all_gather | solution.py:14
  255.4 5.2 %all-gather.17 = f32[4,2,16]{2,1,0:T(2,128)S(1)} all-gather(f32[1,2,16]{2,1,0:T(2,128)S(1)} %bitcast.65), channel_id=11, replica_groups=mesh['expert_0'=4,'expert_1'=4,'dp_0'=8,'dp_1'=2] {'expert_1'}, dimensions={0}, use_global_device_ids=true | all-gather | bytes 640 | tf_op jit(solution)/shard_map/all_gather | solution.py:14
  260.7 10.5 %all-gather.18 = f32[8,2,16]{2,1,0:T(2,128)S(1)} all-gather(f32[1,2,16]{2,1,0:T(2,128)S(1)} %bitcast.66), channel_id=12, replica_groups=mesh['expert_0'=4,'expert_1'=4,'dp_0'=8,'dp_1'=2] {'dp_0'}, dimensions={0}, use_global_device_ids=true | all-gather | bytes 1152 | tf_op jit(solution)/shard_map/all_gather | solution.py:14
  271.2 9.1 %all-gather.19 = f32[2,2,16]{2,1,0:T(2,128)S(1)} all-gather(f32[1,2,16]{2,1,0:T(2,128)S(1)} %bitcast.62), channel_id=13, replica_groups=mesh['expert_0'=4,'expert_1'=4,'dp_0'=8,'dp_1'=2] {'dp_1'}, dimensions={0}, use_global_device_ids=true | all-gather | bytes 384 | tf_op jit(solution)/shard_map/all_gather | solution.py:14
  280.3 0.6 pad_maximum_fusion
  281.0 1.2 fusion.25
  (54 shorter events, 2.4 us)
Async XLA Ops:
  7.2 3.4 %copy-start = (bf16[2,128,1280]{2,1,0:T(8,128)(2,1)S(1)}, bf16[2,128,1280]{2,1,0:T(8,128)(2,1)}, u32[]{:S(2)}) copy-start(bf16[2,128,1280]{2,1,0:T(8,128)(2,1)} %param.6) | copy-start | bytes 1966084
  7.2 12.7 %copy-start.7 = (u32[256]{0:T(256)S(1)}, u32[256]{0:T(256)}, u32[]{:S(2)}) copy-start(u32[256]{0:T(256)} %constant.28) | copy-start | bytes 3076
  7.2 31.6 %copy-start.6 = (u32[256]{0:T(256)S(1)}, u32[256]{0:T(256)}, u32[]{:S(2)}) copy-start(u32[256]{0:T(256)} %constant.33) | copy-start | bytes 3076
  7.2 42.4 %copy-start.5 = (u32[256]{0:T(256)S(1)}, u32[256]{0:T(256)}, u32[]{:S(2)}) copy-start(u32[256]{0:T(256)} %constant.38) | copy-start | bytes 3076
  7.2 62.7 %copy-start.4 = (u32[256]{0:T(256)S(1)}, u32[256]{0:T(256)}, u32[]{:S(2)}) copy-start(u32[256]{0:T(256)} %constant.43) | copy-start | bytes 3076
  7.2 13.9 %copy-start.3 = (s32[2,128]{1,0:T(2,128)S(1)}, s32[2,128]{1,0:T(2,128)}, u32[]{:S(2)}) copy-start(s32[2,128]{1,0:T(2,128)} %param.7) | copy-start | bytes 3076
  7.2 85.3 %all-gather.25.cloned.1.call-start = ((), (), s32[]{:S(2)}) async-start(), calls=%async_computation.3 | async-start | bytes 13926400 | tf_op jit(solution)/shard_map/all_gather | solution.py:52
  8.0 163.0 %all-gather.23.cloned.1.call-start = ((), (), s32[]{:S(2)}) async-start(), calls=%async_computation.2 | async-start | bytes 13926400 | tf_op jit(solution)/shard_map/all_gather | solution.py:46
  12.2 66.9 %all-to-all-start = ((bf16[2,16,16,1280]{3,2,0,1:T(8,128)(2,1)}), bf16[2,16,16,1280]{3,2,0,1:T(8,128)(2,1)S(1)}, u32[]{:S(2)}, u32[]{:S(2)}) async-start(bf16[2,16,16,1280]{3,2,0,1:T(8,128)(2,1)} %copy.23), calls=%async_computation | async-start | bytes 2621440 | tf_op jit(solution)/shard_map/all_to_all | solution.py:42
  193.6 7.8 %copy-start.2 = (s32[2,128,1]{1,2,0:T(1,128)S(1)}, s32[2,128,1]{1,2,0:T(1,128)}, u32[]{:S(2)}) copy-start(s32[2,128,1]{1,2,0:T(1,128)} %param.8) | copy-start | bytes 3076
  193.6 54.6 %copy-start.1 = (bf16[1280,16]{0,1:T(8,128)(2,1)S(1)}, bf16[1280,16]{0,1:T(8,128)(2,1)}, u32[]{:S(2)}) copy-start(bf16[1280,16]{0,1:T(8,128)(2,1)} %param.9) | copy-start | bytes 122884
  194.8 86.1 %all-to-all-start.1 = ((bf16[2,16,16,1280]{3,2,0,1:T(8,128)(2,1)}), bf16[2,16,16,1280]{3,2,0,1:T(8,128)(2,1)S(1)}, u32[]{:S(2)}, u32[]{:S(2)}) async-start(bf16[2,16,16,1280]{3,2,0,1:T(8,128)(2,1)} %copy.25), calls=%async_computation.1 | async-start | bytes 2621440 | tf_op jit(solution)/shard_map/all_to_all | solution.py:56
Sparse Core Ops, SparseCore 0:
  9.9 82.5 all-gather.24
  94.4 76.5 all-gather.22
